TPU v7x, 32 devices: a whole 2x2x4 slice. The times are simulated.
32 devices in a mesh: seq: 4 (over x, core), mp: 8 (over z, y).
Axes of the slice: x: 2, y: 2, z: 4, core: 2. Of those that a mesh axis runs over, the one named last changes fastest.
Arguments:
- byte_states: bfloat16 [4, 4096, 1024], P('seq', 'mp'), may hold values from -312 to 312
- patch_latents: bfloat16 [4, 1024, 4096], P(None, 'seq', 'mp'), may hold values from -6 to 6
- patch_lengths: int32 [4, 1024], P('seq'), may hold values from 1 to 12, 4096 in all within a row
- w_down: bfloat16 [4096, 1024], replicated, may hold values from -0.09375 to 0.09375
- kv_gain: bfloat16 [1024], replicated, may hold values from 0.25 to 1.75
- w_query: bfloat16 [1024, 1024], replicated, may hold values from -0.375 to 0.375
- w_key: bfloat16 [1024, 1024], replicated, may hold values from -0.1875 to 0.1875
- w_value: bfloat16 [1024, 1024], replicated, may hold values from -0.1875 to 0.1875
- w_out: bfloat16 [1024, 1024], replicated, may hold values from -0.375 to 0.375
- out_gain: bfloat16 [1024], replicated, may hold values from 0.25 to 1.75
Outputs:
- decoded: bfloat16 [4, 4096, 1024], P('seq', 'mp')
Inputs may be any that keep to these rules, and one draw needn't show every extreme that they name: patch_lengths[s] lists the lengths of the 1024 patches of sequence s in order; they sum to 4096 and the longest is exactly 12.
All inputs are finite; a program needn't handle non-finite values.
Results may differ from a plain program's by a relative error of at most 0.0076.
Values may be sent and summed in bfloat16 or wider, within the bound.
A program may use at most 128 MiB of HBM per device.

v0:
```python
import math
import jax
import jax.numpy as jnp
from jax import lax
from jax.sharding import PartitionSpec as P

HEADS = 16
HEAD_DIM = 64
NEG_FLOOR = -1e30


def rms_norm(values, gain_row):
    mean_square = jnp.mean(values * values, axis=-1, keepdims=True)
    return values * lax.rsqrt(mean_square + 1e-05) * gain_row.astype(jnp.float32)


def fold_block(fold_state, query_part, position_part, key_block, value_block, start_block):
    row_max, denominator, accumulated = fold_state
    scale_factor = 1.0 / math.sqrt(HEAD_DIM)
    scores = (
        jnp.einsum("rhd,khd->hrk", query_part, key_block, preferred_element_type=jnp.float32)
        * scale_factor
    )
    allowed = start_block[None, None, :] <= position_part[None, :, None]
    masked = jnp.where(allowed, scores, NEG_FLOOR)
    new_max = jnp.maximum(row_max, jnp.max(masked, axis=-1))
    raised = jnp.where(allowed, jnp.exp(masked - new_max[..., None]), 0.0)
    correction = jnp.exp(row_max - new_max)
    denominator = denominator * correction + jnp.sum(raised, axis=-1)
    accumulated = accumulated * correction[..., None] + jnp.einsum(
        "hrk,khd->hrd", raised.astype(jnp.bfloat16), value_block, preferred_element_type=jnp.float32
    )
    return (new_max, denominator, accumulated)


def make_folder(query_halves, position_halves, starts):

    def folder(running, arrived_piece, piece_start):
        key_piece, value_piece = arrived_piece
        piece_rows = key_piece.shape[0]
        step_rows = math.gcd(piece_rows, 512)

        def one_block(block_index, fold_state):
            offset = block_index * step_rows
            key_block = lax.dynamic_slice_in_dim(key_piece, offset, step_rows, 0).reshape(
                step_rows, HEADS, HEAD_DIM
            )
            value_block = lax.dynamic_slice_in_dim(value_piece, offset, step_rows, 0).reshape(
                step_rows, HEADS, HEAD_DIM
            )
            start_block = lax.dynamic_slice_in_dim(starts, offset, step_rows, 0)
            updated = []
            for part_index in range(2):
                part_state = tuple((member[part_index] for member in fold_state))

                def advance(inner_state, part_index=part_index):
                    return fold_block(
                        inner_state,
                        query_halves[part_index],
                        position_halves[part_index],
                        key_block,
                        value_block,
                        start_block,
                    )

                def remain(inner_state):
                    return inner_state

                needed = start_block[0] <= position_halves[part_index][-1]
                updated.append(lax.cond(needed, advance, remain, part_state))
            return tuple((jnp.stack([updated[0][slot], updated[1][slot]]) for slot in range(3)))

        return lax.fori_loop(0, piece_rows // step_rows, one_block, running)

    return folder


def per_device(
    byte_states,
    patch_latents,
    patch_lengths,
    w_down,
    kv_gain,
    w_query,
    w_key,
    w_value,
    w_out,
    out_gain,
):
    my_rank = lax.axis_index("mp")
    tokens_here = byte_states.shape[1]
    half_rows = tokens_here // 2
    regrouped = lax.all_to_all(
        lax.all_to_all(patch_latents, "seq", split_axis=0, concat_axis=1, tiled=True),
        "mp",
        split_axis=1,
        concat_axis=2,
        tiled=True,
    )
    projected = jnp.dot(regrouped[0], w_down, preferred_element_type=jnp.float32)
    patch_normed = rms_norm(projected, kv_gain).astype(jnp.bfloat16)
    lengths = patch_lengths[0]
    starts = jnp.cumsum(lengths) - lengths
    own_rows = byte_states[0]
    local_offsets = jnp.arange(half_rows, dtype=jnp.int32)
    first_position = my_rank * tokens_here
    position_halves = jnp.stack(
        [first_position + local_offsets, first_position + half_rows + local_offsets]
    )
    queries = jnp.dot(own_rows, w_query, preferred_element_type=jnp.float32).astype(jnp.bfloat16)
    query_halves = queries.reshape(2, half_rows, HEADS, HEAD_DIM)
    initial = (
        jnp.full((2, HEADS, half_rows), NEG_FLOOR, jnp.float32),
        jnp.zeros((2, HEADS, half_rows), jnp.float32),
        jnp.zeros((2, HEADS, half_rows, HEAD_DIM), jnp.float32),
    )
    key_rows = jnp.dot(patch_normed, w_key, preferred_element_type=jnp.float32).astype(jnp.bfloat16)
    value_rows = jnp.dot(patch_normed, w_value, preferred_element_type=jnp.float32).astype(
        jnp.bfloat16
    )
    folder = make_folder(query_halves, position_halves, starts)
    row_max, denominator, accumulated = folder(
        initial,
        (
            lax.all_gather(key_rows, "mp", axis=0, tiled=True),
            lax.all_gather(value_rows, "mp", axis=0, tiled=True),
        ),
        jnp.int32(0),
    )
    summed = accumulated / denominator[..., None]
    head_out = (
        jnp.transpose(summed, (0, 2, 1, 3))
        .reshape(tokens_here, HEADS * HEAD_DIM)
        .astype(jnp.bfloat16)
    )
    residual = own_rows.astype(jnp.float32) + jnp.dot(
        head_out, w_out, preferred_element_type=jnp.float32
    )
    decoded = rms_norm(residual, out_gain).astype(jnp.bfloat16)
    return decoded[None]


def solution(mesh):
    return jax.shard_map(
        per_device,
        mesh=mesh,
        in_specs=(
            P("seq", "mp", None),
            P(None, "seq", "mp"),
            P("seq", None),
            P(),
            P(),
            P(),
            P(),
            P(),
            P(),
            P(),
        ),
        out_specs=P("seq", "mp", None),
        check_vma=False,
    )
```

profile of v0, /device:TPU:16, one launch (start us, length us, event | category | flops | bytes accessed | tf_op | source)
XLA Modules:
  0.0 283.9 jit_solution(9395675272807082795)
XLA Ops:
  6.5 18.0 %all_to_all.27 = bf16[4,256,512]{2,1,0:T(8,128)(2,1)S(1)} all-to-all(bf16[4,256,512]{2,1,0:T(8,128)(2,1)} %param.17), channel_id=1, replica_groups=mesh['seq'=4,'mp'=8] {'seq'}, dimensions={0} | all-to-all | bytes 2097152 | tf_op jit(solution)/shard_map/all_to_all | solution.py:94
  24.6 3.0 %copy.45 = bf16[1,1024,512]{2,0,1:T(2,128)(2,1)} copy(bf16[1,1024,512]{2,1,0:T(8,128)(2,1)S(1)} %bitcast.101) | data formatting | bytes 2097152 | tf_op jit(solution)/shard_map/all_to_all | solution.py:94
  28.1 8.0 %reduce.2 = bf16[1024,512]{1,0:T(8,128)(2,1)S(1)} reduce(bf16[1024,1,512]{2,1,0:T(2,128)(2,1)} %bitcast.98, bf16[]{:T(256)} %broadcast.104), dimensions={1}, to_apply=%bitcast.78.reduce_sub_computation | reduce | bytes 2097154
  36.1 1.6 reshape.138
  37.7 6.2 %all-to-all-start.1 = ((bf16[8,2,32768]{2,1,0:T(2,128)(2,1)}), bf16[8,2,32768]{2,1,0:T(2,128)(2,1)S(1)}, u32[]{:S(2)}, u32[]{:S(2)}) async-start(bf16[8,2,32768]{2,1,0:T(2,128)(2,1)} %reshape.138), calls=%async_computation.1 | async-start | bytes 2097152 | tf_op jit(solution)/shard_map/all_to_all | solution.py:93
  43.9 22.3 %all-to-all-done.1 = bf16[8,2,32768]{2,1,0:T(2,128)(2,1)S(1)} async-done(((bf16[8,2,32768]{2,1,0:T(2,128)(2,1)}), bf16[8,2,32768]{2,1,0:T(2,128)(2,1)S(1)}, u32[]{:S(2)}, u32[]{:S(2)}) %all-to-all-start.1) | async-done | bytes 1048608 | tf_op jit(solution)/shard_map/all_to_all | solution.py:93
  66.1 3.4 %reshape.139 = bf16[1024,1,512]{2,1,0:T(2,128)(2,1)} reshape(bf16[8,2,32768]{2,1,0:T(2,128)(2,1)S(1)} %all-to-all-done.1) | data formatting | bytes 2097152
  69.6 2.8 %copy.42 = bf16[1,1024,512]{2,1,0:T(8,128)(2,1)} copy(bf16[1,1024,512]{2,0,1:T(2,128)(2,1)} %bitcast.97) | data formatting | bytes 2097152
  72.4 1.6 copy.32
  74.0 4.9 %multiply_reduce_fusion.1 = (f32[128]{0:T(128)S(1)}, f32[128,1024]{1,0:T(8,128)S(1)}) fusion(bf16[128,4096]{0,1:T(8,128)(2,1)S(1)} %bitcast.99, bf16[4096,1024]{1,0:T(8,128)(2,1)} %param.19), kind=kOutput, calls=%fused_computation.58 | convolution fusion | flops 1074003840 | bytes 9961984 | tf_op jit(solution)/shard_map/dot_general | solution.py:100
  79.7 1.2 convolution_convert_fusion.2
  81.2 3.0 %convolution_convert_fusion.1 = bf16[128,1024]{1,0:T(8,128)(2,1)} fusion(bf16[1024,1024]{1,0:T(8,128)(2,1)} %param.23, f32[128,1024]{1,0:T(8,128)} %copy-done.7, f32[1024]{0:T(1024)S(1)} %convert_element_type.60, f32[128]{0:T(128)S(1)} %add_rsqrt_fusion.1), kind=kOutput, calls=%fused_computation.52 | convolution fusion | flops 268959744 | bytes 2888192 | tf_op jit(solution)/shard_map/dot_general | solution.py:118
  84.6 3.2 %convolution_convert_fusion = bf16[512,1024]{1,0:T(8,128)(2,1)S(1)} fusion(bf16[1024,1024]{1,0:T(8,128)(2,1)} %param.21, bf16[1,512,1024]{2,1,0:T(8,128)(2,1)} %param.16), kind=kOutput, calls=%fused_computation.51 | convolution fusion | flops 1074266112 | bytes 4194304 | tf_op jit(solution)/shard_map/dot_general | solution.py:110
  87.7 2.4 reshape.136
  90.1 3.6 %copy.36 = bf16[2,256,16,64]{1,3,2,0:T(8,128)(2,1)} copy(bf16[2,256,16,64]{3,2,1,0:T(8,128)(2,1)} %reshape.136) | data formatting | bytes 2097152 | tf_op jit(solution)/shard_map/while | solution.py:73
  93.8 36.8 %all-gather.3.cloned.1.call-done = bf16[1024,1024]{1,0:T(8,128)(2,1)} async-done(((bf16[128,1024]{1,0:T(8,128)(2,1)}), bf16[1024,1024]{1,0:T(8,128)(2,1)}) %all-gather.3.cloned.1.call-update) | async-done | bytes 2097168 | tf_op jit(solution)/shard_map/all_gather | solution.py:125
  130.6 49.8 %all-gather.5.cloned.1.call-done = bf16[1024,1024]{1,0:T(8,128)(2,1)} async-done(((bf16[128,1024]{1,0:T(8,128)(2,1)}), bf16[1024,1024]{1,0:T(8,128)(2,1)}) %all-gather.5.cloned.1.call-update) | async-done | bytes 2097168 | tf_op jit(solution)/shard_map/all_gather | solution.py:126
  180.4 1.6 broadcast_in_dim.57
  182.0 88.0 %while.17 = (s32[]{:T(128)}, f32[2,16,256]{2,1,0:T(8,128)S(1)}, f32[2,16,256]{2,1,0:T(8,128)S(1)}, f32[2,16,256,64]{2,3,1,0:T(8,128)}, s32[1024]{0:T(1024)S(1)},...) while((s32[]{:T(128)}, f32[2,16,256]{2,1,0:T(8,128)S(1)}, ...), condition=%wide.region_12.13_spmd, body=%wide.region_3.12_spmd.sunk | while | flops 1130135552 | bytes 103557752 | solution.py:73
  185.2 3.1 %slice_bitcast_fusion.9 = (f32[16,256,64]{1,2,0:T(8,128)}, f32[16,256,64]{1,2,0:T(8,128)}) fusion(f32[2,16,256,64]{2,3,1,0:T(8,128)} %get-tuple-element.503), kind=kLoop, calls=%fused_computation.38.clone.1 | loop fusion | bytes 4194304 | tf_op jit(solution)/shard_map/while/body/eval_jaxpr/squeeze | solution.py:54
  188.3 3.0 %constant_dynamic-slice_fusion.3 = (bf16[512,1024]{1,0:T(8,128)(2,1)}, bf16[512,1024]{1,0:T(8,128)(2,1)}) fusion(bf16[1024,1024]{1,0:T(8,128)(2,1)} %get-tuple-element.521, s32[]{:T(128)S(6)} %select_n.71, bf16[1024,1024]{1,0:T(8,128)(2,1)} %get-tuple-element.520), kind=kLoop, calls=%fused_computation.45.clone.1 | loop fusion | bytes 4194308 | tf_op jit(solution)/shard_map/while/body/eval_jaxpr/dynamic_slice | solution.py:48
  191.3 1.5 copy.48
  193.5 2.3 copy.49
  195.8 11.8 %conditional.4 = (f32[1,16,256]{2,1,0:T(8,128)}, f32[1,16,256]{2,1,0:T(8,128)S(1)}, f32[1,16,256,64]{2,3,1,0:T(8,128)}) conditional(s32[]{:T(128)} %bitcast.87, (f32[16,256]{1,0:T(8,128)}, f32[16,256]{1,0:T(8,128)S(1)}, f32[16,256,64]{1,2,0:T(8,128)}) %tuple.129, (s32[512]{0:T(512)S(1)}, s32[256]{0:T(256)S(1)}, bf16[2,256,16,64]{1,3,2,0:T(8,128)(2,1)}, ...), branch_computations={%region_8.8_spmd, %region_9.0_spmd} | conditional | flops 564797440 | bytes 43224172 | solution.py:70
  196.0 2.9 %fusion.18 = (f32[16,256]{1,0:T(8,128)S(1)}, f32[16,256,512]{2,1,0:T(8,128)S(1)}) fusion(pred[256,512]{1,0:T(8,128)(4,1)S(1)} %broadcast_compare_fusion.1, bf16[512,16,64]{0,2,1:T(8,128)(2,1)S(1)} %get-tuple-element.254, bf16[2,256,16,64]{1,3,2,0:T(8,128)(2,1)} %get-tuple-element.253), kind=kOutput, calls=%fused_computation.20 | convolution fusion | flops 274722816 | bytes 10108928 | tf_op jit(solution)/shard_map/while/body/eval_jaxpr/cond/branch_1_fun/rhd,khd->hrk/dot_general | solution.py:21
  199.5 3.2 %fusion.20 = f32[16,256]{1,0:T(8,128)S(1)} fusion(f32[16,256,512]{2,1,0:T(8,128)S(1)} %get-tuple-element.368, f32[16,256]{1,0:T(8,128)} %max.5, pred[256,512]{1,0:T(8,128)(4,1)S(1)} %broadcast_compare_fusion.1), kind=kLoop, calls=%fused_computation.22 | loop fusion | flops 10481664 | bytes 8552448 | tf_op jit(solution)/shard_map/while/body/eval_jaxpr/cond/branch_1_fun/reduce_sum | solution.py:29
  203.5 3.1 %fusion.27 = f32[1,16,256,64]{2,3,1,0:T(8,128)S(1)} fusion(bf16[512,16,64]{0,2,1:T(8,128)(2,1)S(1)} %copy-done.5, f32[16,256,512]{2,1,0:T(8,128)S(1)} %get-tuple-element.368, f32[16,256]{1,0:T(8,128)} %max.5, pred[256,512]{1,0:T(8,128)(4,1)S(1)} %broadcast_compare_fusion.1, f32[16,256,64]{1,2,0:T(8,128)S(1)} %copy-done.3, f32[16,256]{1,0:T(8,128)S(1)} %get-tuple-element.364), kind=kOutput, calls=%fused_computation.26 | convolution fusion | flops 279445504 | bytes 11698176 | tf_op jit(solution)/shard_map/while/body/eval_jaxpr/cond/branch_1_fun/hrk,khd->hrd/dot_general | solution.py:30
  210.3 11.8 %conditional.5 = (f32[1,16,256]{2,1,0:T(8,128)}, f32[1,16,256]{2,1,0:T(8,128)S(1)}, f32[1,16,256,64]{2,3,1,0:T(8,128)}) conditional(s32[]{:T(128)} %bitcast.90, (f32[16,256]{1,0:T(8,128)}, f32[16,256]{1,0:T(8,128)S(1)}, f32[16,256,64]{1,2,0:T(8,128)}) %tuple.131, (s32[512]{0:T(512)S(1)}, s32[256]{0:T(256)S(1)}, bf16[2,256,16,64]{1,3,2,0:T(8,128)(2,1)}, ...), branch_computations={%region_4.4_spmd, %region_5.0_spmd} | conditional | flops 564797440 | bytes 43224172 | solution.py:70
  210.5 2.9 %fusion = (f32[16,256]{1,0:T(8,128)S(1)}, f32[16,256,512]{2,1,0:T(8,128)S(1)}) fusion(pred[256,512]{1,0:T(8,128)(4,1)S(1)} %broadcast_compare_fusion, bf16[512,16,64]{0,2,1:T(8,128)(2,1)S(1)} %get-tuple-element.246, bf16[2,256,16,64]{1,3,2,0:T(8,128)(2,1)} %get-tuple-element.245), kind=kOutput, calls=%fused_computation.2 | convolution fusion | flops 274722816 | bytes 10108928 | tf_op jit(solution)/shard_map/while/body/eval_jaxpr/cond/branch_1_fun/rhd,khd->hrk/dot_general | solution.py:21
  214.0 3.2 %fusion.2 = f32[16,256]{1,0:T(8,128)S(1)} fusion(f32[16,256,512]{2,1,0:T(8,128)S(1)} %get-tuple-element.366, f32[16,256]{1,0:T(8,128)} %max.4, pred[256,512]{1,0:T(8,128)(4,1)S(1)} %broadcast_compare_fusion), kind=kLoop, calls=%fused_computation.4 | loop fusion | flops 10481664 | bytes 8552448 | tf_op jit(solution)/shard_map/while/body/eval_jaxpr/cond/branch_1_fun/reduce_sum | solution.py:29
  218.0 3.1 %fusion.9 = f32[1,16,256,64]{2,3,1,0:T(8,128)S(1)} fusion(bf16[512,16,64]{0,2,1:T(8,128)(2,1)S(1)} %copy-done.6, f32[16,256,512]{2,1,0:T(8,128)S(1)} %get-tuple-element.366, f32[16,256]{1,0:T(8,128)} %max.4, pred[256,512]{1,0:T(8,128)(4,1)S(1)} %broadcast_compare_fusion, f32[16,256,64]{1,2,0:T(8,128)S(1)} %copy-done.1, f32[16,256]{1,0:T(8,128)S(1)} %get-tuple-element.362), kind=kOutput, calls=%fused_computation.8 | convolution fusion | flops 279445504 | bytes 11698176 | tf_op jit(solution)/shard_map/while/body/eval_jaxpr/cond/branch_1_fun/hrk,khd->hrd/dot_general | solution.py:30
  222.9 3.1 %pad_maximum_fusion.8 = f32[2,16,256,64]{2,3,1,0:T(8,128)} fusion(f32[1,16,256,64]{2,3,1,0:T(8,128)} %get-tuple-element.472, f32[1,16,256,64]{2,3,1,0:T(8,128)} %get-tuple-element.473), kind=kLoop, calls=%fused_computation.36.clone.1 | loop fusion | flops 524288 | bytes 4194304 | tf_op jit(solution)/shard_map/while/body/eval_jaxpr/stack | solution.py:71
  229.2 3.1 %slice_bitcast_fusion.9 = (f32[16,256,64]{1,2,0:T(8,128)}, f32[16,256,64]{1,2,0:T(8,128)}) fusion(f32[2,16,256,64]{2,3,1,0:T(8,128)} %get-tuple-element.503), kind=kLoop, calls=%fused_computation.38.clone.1 | loop fusion | bytes 4194304 | tf_op jit(solution)/shard_map/while/body/eval_jaxpr/squeeze | solution.py:54
  232.3 3.0 %constant_dynamic-slice_fusion.3 = (bf16[512,1024]{1,0:T(8,128)(2,1)}, bf16[512,1024]{1,0:T(8,128)(2,1)}) fusion(bf16[1024,1024]{1,0:T(8,128)(2,1)} %get-tuple-element.521, s32[]{:T(128)S(6)} %select_n.71, bf16[1024,1024]{1,0:T(8,128)(2,1)} %get-tuple-element.520), kind=kLoop, calls=%fused_computation.45.clone.1 | loop fusion | bytes 4194308 | tf_op jit(solution)/shard_map/while/body/eval_jaxpr/dynamic_slice | solution.py:48
  235.3 1.5 copy.48
  237.5 2.3 copy.49
  239.8 11.8 %conditional.4 = (f32[1,16,256]{2,1,0:T(8,128)}, f32[1,16,256]{2,1,0:T(8,128)S(1)}, f32[1,16,256,64]{2,3,1,0:T(8,128)}) conditional(s32[]{:T(128)} %bitcast.87, (f32[16,256]{1,0:T(8,128)}, f32[16,256]{1,0:T(8,128)S(1)}, f32[16,256,64]{1,2,0:T(8,128)}) %tuple.129, (s32[512]{0:T(512)S(1)}, s32[256]{0:T(256)S(1)}, bf16[2,256,16,64]{1,3,2,0:T(8,128)(2,1)}, ...), branch_computations={%region_8.8_spmd, %region_9.0_spmd} | conditional | flops 564797440 | bytes 43224172 | solution.py:70
  240.0 2.9 %fusion.18 = (f32[16,256]{1,0:T(8,128)S(1)}, f32[16,256,512]{2,1,0:T(8,128)S(1)}) fusion(pred[256,512]{1,0:T(8,128)(4,1)S(1)} %broadcast_compare_fusion.1, bf16[512,16,64]{0,2,1:T(8,128)(2,1)S(1)} %get-tuple-element.254, bf16[2,256,16,64]{1,3,2,0:T(8,128)(2,1)} %get-tuple-element.253), kind=kOutput, calls=%fused_computation.20 | convolution fusion | flops 274722816 | bytes 10108928 | tf_op jit(solution)/shard_map/while/body/eval_jaxpr/cond/branch_1_fun/rhd,khd->hrk/dot_general | solution.py:21
  243.5 3.2 %fusion.20 = f32[16,256]{1,0:T(8,128)S(1)} fusion(f32[16,256,512]{2,1,0:T(8,128)S(1)} %get-tuple-element.368, f32[16,256]{1,0:T(8,128)} %max.5, pred[256,512]{1,0:T(8,128)(4,1)S(1)} %broadcast_compare_fusion.1), kind=kLoop, calls=%fused_computation.22 | loop fusion | flops 10481664 | bytes 8552448 | tf_op jit(solution)/shard_map/while/body/eval_jaxpr/cond/branch_1_fun/reduce_sum | solution.py:29
  247.5 3.1 %fusion.27 = f32[1,16,256,64]{2,3,1,0:T(8,128)S(1)} fusion(bf16[512,16,64]{0,2,1:T(8,128)(2,1)S(1)} %copy-done.5, f32[16,256,512]{2,1,0:T(8,128)S(1)} %get-tuple-element.368, f32[16,256]{1,0:T(8,128)} %max.5, pred[256,512]{1,0:T(8,128)(4,1)S(1)} %broadcast_compare_fusion.1, f32[16,256,64]{1,2,0:T(8,128)S(1)} %copy-done.3, f32[16,256]{1,0:T(8,128)S(1)} %get-tuple-element.364), kind=kOutput, calls=%fused_computation.26 | convolution fusion | flops 279445504 | bytes 11698176 | tf_op jit(solution)/shard_map/while/body/eval_jaxpr/cond/branch_1_fun/hrk,khd->hrd/dot_general | solution.py:30
  254.3 11.8 %conditional.5 = (f32[1,16,256]{2,1,0:T(8,128)}, f32[1,16,256]{2,1,0:T(8,128)S(1)}, f32[1,16,256,64]{2,3,1,0:T(8,128)}) conditional(s32[]{:T(128)} %bitcast.90, (f32[16,256]{1,0:T(8,128)}, f32[16,256]{1,0:T(8,128)S(1)}, f32[16,256,64]{1,2,0:T(8,128)}) %tuple.131, (s32[512]{0:T(512)S(1)}, s32[256]{0:T(256)S(1)}, bf16[2,256,16,64]{1,3,2,0:T(8,128)(2,1)}, ...), branch_computations={%region_4.4_spmd, %region_5.0_spmd} | conditional | flops 564797440 | bytes 43224172 | solution.py:70
  254.5 2.9 %fusion = (f32[16,256]{1,0:T(8,128)S(1)}, f32[16,256,512]{2,1,0:T(8,128)S(1)}) fusion(pred[256,512]{1,0:T(8,128)(4,1)S(1)} %broadcast_compare_fusion, bf16[512,16,64]{0,2,1:T(8,128)(2,1)S(1)} %get-tuple-element.246, bf16[2,256,16,64]{1,3,2,0:T(8,128)(2,1)} %get-tuple-element.245), kind=kOutput, calls=%fused_computation.2 | convolution fusion | flops 274722816 | bytes 10108928 | tf_op jit(solution)/shard_map/while/body/eval_jaxpr/cond/branch_1_fun/rhd,khd->hrk/dot_general | solution.py:21
  258.0 3.2 %fusion.2 = f32[16,256]{1,0:T(8,128)S(1)} fusion(f32[16,256,512]{2,1,0:T(8,128)S(1)} %get-tuple-element.366, f32[16,256]{1,0:T(8,128)} %max.4, pred[256,512]{1,0:T(8,128)(4,1)S(1)} %broadcast_compare_fusion), kind=kLoop, calls=%fused_computation.4 | loop fusion | flops 10481664 | bytes 8552448 | tf_op jit(solution)/shard_map/while/body/eval_jaxpr/cond/branch_1_fun/reduce_sum | solution.py:29
  262.0 3.1 %fusion.9 = f32[1,16,256,64]{2,3,1,0:T(8,128)S(1)} fusion(bf16[512,16,64]{0,2,1:T(8,128)(2,1)S(1)} %copy-done.6, f32[16,256,512]{2,1,0:T(8,128)S(1)} %get-tuple-element.366, f32[16,256]{1,0:T(8,128)} %max.4, pred[256,512]{1,0:T(8,128)(4,1)S(1)} %broadcast_compare_fusion, f32[16,256,64]{1,2,0:T(8,128)S(1)} %copy-done.1, f32[16,256]{1,0:T(8,128)S(1)} %get-tuple-element.362), kind=kOutput, calls=%fused_computation.8 | convolution fusion | flops 279445504 | bytes 11698176 | tf_op jit(solution)/shard_map/while/body/eval_jaxpr/cond/branch_1_fun/hrk,khd->hrd/dot_general | solution.py:30
  266.9 3.1 %pad_maximum_fusion.8 = f32[2,16,256,64]{2,3,1,0:T(8,128)} fusion(f32[1,16,256,64]{2,3,1,0:T(8,128)} %get-tuple-element.472, f32[1,16,256,64]{2,3,1,0:T(8,128)} %get-tuple-element.473), kind=kLoop, calls=%fused_computation.36.clone.1 | loop fusion | flops 524288 | bytes 4194304 | tf_op jit(solution)/shard_map/while/body/eval_jaxpr/stack | solution.py:71
  270.0 1.8 fusion.38
  273.2 2.6 multiply_reduce_fusion
  275.8 1.2 fusion.36
  (85 shorter events, 22.8 us)
Async XLA Ops:
  6.5 266.6 %copy-start = (bf16[1024,1024]{1,0:T(8,128)(2,1)S(1)}, bf16[1024,1024]{1,0:T(8,128)(2,1)}, u32[]{:S(2)}) copy-start(bf16[1024,1024]{1,0:T(8,128)(2,1)} %param.24) | copy-start | bytes 6291460
  6.5 37.3 %copy-start.10 = (bf16[1024]{0:T(1024)(128)(2,1)S(1)}, bf16[1024]{0:T(1024)(128)(2,1)}, u32[]{:S(2)}) copy-start(bf16[1024]{0:T(1024)(128)(2,1)} %param.20) | copy-start | bytes 6148
  37.7 28.5 %all-to-all-start.1 = ((bf16[8,2,32768]{2,1,0:T(2,128)(2,1)}), bf16[8,2,32768]{2,1,0:T(2,128)(2,1)S(1)}, u32[]{:S(2)}, u32[]{:S(2)}) async-start(bf16[8,2,32768]{2,1,0:T(2,128)(2,1)} %reshape.138), calls=%async_computation.1 | async-start | bytes 2097152 | tf_op jit(solution)/shard_map/all_to_all | solution.py:93
  43.9 86.8 %all-gather.3.cloned.1.call-start = ((), (), s32[]{:S(2)}) async-start(), calls=%async_computation.2 | async-start | bytes 2359296 | tf_op jit(solution)/shard_map/all_gather | solution.py:125
  74.0 5.7 %copy-start.8 = (bf16[1024,1024]{1,0:T(8,128)(2,1)S(1)}, bf16[1024,1024]{1,0:T(8,128)(2,1)}, u32[]{:S(2)}) copy-start(bf16[1024,1024]{1,0:T(8,128)(2,1)} %param.22) | copy-start | bytes 6291460
  74.0 10.1 %copy-start.9 = (s32[1,1024]{1,0:T(1,128)S(1)}, s32[1,1024]{1,0:T(1,128)}, u32[]{:S(2)}) copy-start(s32[1,1024]{1,0:T(1,128)} %param.18) | copy-start | bytes 12292
  78.9 0.8 copy-start.7
  80.9 12.7 %copy-start.11 = (bf16[1024]{0:T(1024)(128)(2,1)S(1)}, bf16[1024]{0:T(1024)(128)(2,1)}, u32[]{:S(2)}) copy-start(bf16[1024]{0:T(1024)(128)(2,1)} %param.25) | copy-start | bytes 6148
  80.9 99.5 %all-gather.5.cloned.1.call-start = ((), (), s32[]{:S(2)}) async-start(), calls=%async_computation.3 | async-start | bytes 2359296 | tf_op jit(solution)/shard_map/all_gather | solution.py:126
  195.9 7.5 %copy-start.3 = (f32[16,256,64]{1,2,0:T(8,128)S(1)}, f32[16,256,64]{1,2,0:T(8,128)}, u32[]{:S(2)}) copy-start(f32[16,256,64]{1,2,0:T(8,128)} %get-tuple-element.256) | copy-start | bytes 3145732 | tf_op jit(solution)/shard_map/while/body/eval_jaxpr/cond
  196.0 7.5 %copy-start.5 = (bf16[512,16,64]{0,2,1:T(8,128)(2,1)S(1)}, bf16[512,16,64]{0,2,1:T(8,128)(2,1)}, u32[]{:S(2)}) copy-start(bf16[512,16,64]{0,2,1:T(8,128)(2,1)} %get-tuple-element.257) | copy-start | bytes 3145732 | tf_op jit(solution)/shard_map/while/body/eval_jaxpr/cond
  206.6 1.0 copy-start.4
  210.5 7.5 %copy-start.1 = (f32[16,256,64]{1,2,0:T(8,128)S(1)}, f32[16,256,64]{1,2,0:T(8,128)}, u32[]{:S(2)}) copy-start(f32[16,256,64]{1,2,0:T(8,128)} %get-tuple-element.248) | copy-start | bytes 3145732 | tf_op jit(solution)/shard_map/while/body/eval_jaxpr/cond
  210.5 7.5 %copy-start.6 = (bf16[512,16,64]{0,2,1:T(8,128)(2,1)S(1)}, bf16[512,16,64]{0,2,1:T(8,128)(2,1)}, u32[]{:S(2)}) copy-start(bf16[512,16,64]{0,2,1:T(8,128)(2,1)} %get-tuple-element.249) | copy-start | bytes 3145732 | tf_op jit(solution)/shard_map/while/body/eval_jaxpr/cond
  221.2 1.0 copy-start.2
  240.0 7.5 %copy-start.3 = (f32[16,256,64]{1,2,0:T(8,128)S(1)}, f32[16,256,64]{1,2,0:T(8,128)}, u32[]{:S(2)}) copy-start(f32[16,256,64]{1,2,0:T(8,128)} %get-tuple-element.256) | copy-start | bytes 3145732 | tf_op jit(solution)/shard_map/while/body/eval_jaxpr/cond
  240.0 7.5 %copy-start.5 = (bf16[512,16,64]{0,2,1:T(8,128)(2,1)S(1)}, bf16[512,16,64]{0,2,1:T(8,128)(2,1)}, u32[]{:S(2)}) copy-start(bf16[512,16,64]{0,2,1:T(8,128)(2,1)} %get-tuple-element.257) | copy-start | bytes 3145732 | tf_op jit(solution)/shard_map/while/body/eval_jaxpr/cond
  250.7 1.0 copy-start.4
  254.5 7.5 %copy-start.1 = (f32[16,256,64]{1,2,0:T(8,128)S(1)}, f32[16,256,64]{1,2,0:T(8,128)}, u32[]{:S(2)}) copy-start(f32[16,256,64]{1,2,0:T(8,128)} %get-tuple-element.248) | copy-start | bytes 3145732 | tf_op jit(solution)/shard_map/while/body/eval_jaxpr/cond
  254.5 7.5 %copy-start.6 = (bf16[512,16,64]{0,2,1:T(8,128)(2,1)S(1)}, bf16[512,16,64]{0,2,1:T(8,128)(2,1)}, u32[]{:S(2)}) copy-start(bf16[512,16,64]{0,2,1:T(8,128)(2,1)} %get-tuple-element.249) | copy-start | bytes 3145732 | tf_op jit(solution)/shard_map/while/body/eval_jaxpr/cond
  265.2 1.0 copy-start.2
Sparse Core Ops, SparseCore 0:
  81.1 49.5 all-gather.2
  132.7 47.6 all-gather.4
where the time goes:
time: 286 us; the launch traced here: 284 us
  waiting for transfers between devices  109 us (38%)
  local copies, waits for them, and re-layouts  54.5 us (19%)
  matrix products  39.1 us (14%)
  other arithmetic  38 us (13%)
  blocking collectives  18 us (6%)
  between operations  13.5 us (5%)
  starting transfers between devices  6.39 us (2%)
  loops' own time  5.51 us (2%)
    all_gather x1, waiting for transfers between devices, per_device(): lax.all_gather(value_rows, 'mp', axis=0, tiled=True)  49.8 us
    all_gather x1, waiting for transfers between devices, per_device(): lax.all_gather(key_rows, 'mp', axis=0, tiled=True)  36.8 us
    all_to_all x1, waiting for transfers between devices, per_device(): lax.all_to_all(lax.all_to_all(patch_latents, 'seq', split_axis=0, concat_...  22.3 us
    all_to_all x1, blocking collectives, per_device(): lax.all_to_all(patch_latents, 'seq', split_axis=0, concat_axis=1, tiled=T...  18 us
    reduce_sum x4, other arithmetic, fold_block(): denominator = denominator * correction + jnp.sum(raised, axis=-1)  12.9 us
    dot_general x4, matrix products, fold_block(): jnp.einsum('hrk,khd->hrd', raised.astype(jnp.bfloat16), value_block, pref...  12.6 us
    dot_general x4, matrix products, fold_block(): jnp.einsum('rhd,khd->hrk', query_part, key_block, preferred_element_type=...  11.7 us
    another operation x10, other arithmetic, one_block(): jnp.stack([updated[0][slot], updated[1][slot]])  10.6 us
  transfers between devices with their start and end apart: 3, of which 3 were waited for; matrix products, arithmetic and copies ran while one was open for 4% of the time, Pallas kernels for 0%

commit v1 on v0

--- a/solution.py
+++ b/solution.py
@@ -3,6 +3,7 @@
 import jax.numpy as jnp
 from jax import lax
 from jax.sharding import PartitionSpec as P
+from jax.lax import all_to_all, axis_size
 
 HEADS = 16
 HEAD_DIM = 64
@@ -91,7 +92,15 @@
     tokens_here = byte_states.shape[1]
     half_rows = tokens_here // 2
     regrouped = lax.all_to_all(
-        lax.all_to_all(patch_latents, "seq", split_axis=0, concat_axis=1, tiled=True),
+        jnp.concatenate(
+            all_to_all(
+                jnp.stack(jnp.split(patch_latents, axis_size("seq"), 0), 0),
+                axis_name="seq",
+                split_axis=0,
+                concat_axis=0,
+            ),
+            1,
+        ),
         "mp",
         split_axis=1,
         concat_axis=2,

time: 286 us -> 286 us (level)
    all_to_all x2 -> x1, local copies, waits for them, and re-layouts: 4.58 us -> 1.61 us  [per_device(): lax.all_to_all(jnp.concatenate(all_to_all(jnp.stack(jnp.split(patch_laten...]
    reshape x0 -> x1, local copies, waits for them, and re-layouts: none -> 2.96 us  [per_device(): jnp.concatenate(all_to_all(jnp.stack(jnp.split(patch_latents, axis_size('...]
where the time goes in v1:
time: 286 us; the launch traced here: 284 us
  waiting for transfers between devices  109 us (38%)
  local copies, waits for them, and re-layouts  55.7 us (19%)
  matrix products  39.1 us (14%)
  other arithmetic  38.1 us (13%)
  blocking collectives  17 us (6%)
  between operations  13.5 us (5%)
  starting transfers between devices  6.39 us (2%)
  loops' own time  5.07 us (2%)
    all_gather x1, waiting for transfers between devices, per_device(): lax.all_gather(value_rows, 'mp', axis=0, tiled=True)  49.8 us
    all_gather x1, waiting for transfers between devices, per_device(): lax.all_gather(key_rows, 'mp', axis=0, tiled=True)  36.8 us
    all_to_all x1, waiting for transfers between devices, per_device(): lax.all_to_all(jnp.concatenate(all_to_all(jnp.stack(jnp.split(patch_laten...  22.3 us
    all_to_all x1, blocking collectives, per_device(): all_to_all(jnp.stack(jnp.split(patch_latents, axis_size('seq'), 0), 0), a...  17 us
    reduce_sum x4, other arithmetic, fold_block(): denominator = denominator * correction + jnp.sum(raised, axis=-1)  12.9 us
    dot_general x4, matrix products, fold_block(): jnp.einsum('hrk,khd->hrd', raised.astype(jnp.bfloat16), value_block, pref...  12.6 us
    dot_general x4, matrix products, fold_block(): jnp.einsum('rhd,khd->hrk', query_part, key_block, preferred_element_type=...  11.7 us
    another operation x10, other arithmetic, one_block(): jnp.stack([updated[0][slot], updated[1][slot]])  10.6 us
  transfers between devices with their start and end apart: 3, of which 3 were waited for; matrix products, arithmetic and copies ran while one was open for 4% of the time, Pallas kernels for 0%

profile of v1, /device:TPU:16, one launch (start us, length us, event | category | flops | bytes accessed | tf_op | source)
XLA Modules:
  0.0 283.8 jit_solution(10535084629590974657)
XLA Ops:
  6.5 1.4 slice_bitcast_fusion.9
  8.1 17.0 %all_to_all.20 = bf16[4,1,256,512]{3,2,1,0:T(8,128)(2,1)S(1)} all-to-all(bf16[4,1,256,512]{3,2,1,0:T(8,128)(2,1)S(1)} %pad_maximum_fusion.3), channel_id=1, replica_groups=mesh['seq'=4,'mp'=8] {'seq'}, dimensions={0} | all-to-all | bytes 2097152 | tf_op jit(solution)/shard_map/all_to_all | solution.py:96
  25.1 3.0 %copy.52 = bf16[1,1024,512]{2,0,1:T(2,128)(2,1)} copy(bf16[1,1024,512]{2,1,0:T(8,128)(2,1)S(1)} %bitcast.108) | data formatting | bytes 2097152 | tf_op jit(solution)/shard_map/reshape | solution.py:95
  28.6 8.0 %reduce.2 = bf16[1024,512]{1,0:T(8,128)(2,1)S(1)} reduce(bf16[1024,1,512]{2,1,0:T(2,128)(2,1)} %bitcast.106, bf16[]{:T(256)} %broadcast.104), dimensions={1}, to_apply=%bitcast.86.reduce_sub_computation | reduce | bytes 2097154
  36.6 1.6 reshape.139
  38.2 6.2 %all-to-all-start.1 = ((bf16[8,2,32768]{2,1,0:T(2,128)(2,1)}), bf16[8,2,32768]{2,1,0:T(2,128)(2,1)S(1)}, u32[]{:S(2)}, u32[]{:S(2)}) async-start(bf16[8,2,32768]{2,1,0:T(2,128)(2,1)} %reshape.139), calls=%async_computation.1 | async-start | bytes 2097152 | tf_op jit(solution)/shard_map/all_to_all | solution.py:94
  44.4 22.3 %all-to-all-done.1 = bf16[8,2,32768]{2,1,0:T(2,128)(2,1)S(1)} async-done(((bf16[8,2,32768]{2,1,0:T(2,128)(2,1)}), bf16[8,2,32768]{2,1,0:T(2,128)(2,1)S(1)}, u32[]{:S(2)}, u32[]{:S(2)}) %all-to-all-start.1) | async-done | bytes 1048608 | tf_op jit(solution)/shard_map/all_to_all | solution.py:94
  66.6 3.4 %reshape.140 = bf16[1024,1,512]{2,1,0:T(2,128)(2,1)} reshape(bf16[8,2,32768]{2,1,0:T(2,128)(2,1)S(1)} %all-to-all-done.1) | data formatting | bytes 2097152
  70.1 2.8 %copy.49 = bf16[1,1024,512]{2,1,0:T(8,128)(2,1)} copy(bf16[1,1024,512]{2,0,1:T(2,128)(2,1)} %bitcast.105) | data formatting | bytes 2097152
  72.9 1.6 copy.39
  74.6 4.9 %multiply_reduce_fusion.1 = (f32[128]{0:T(128)S(1)}, f32[128,1024]{1,0:T(8,128)S(1)}) fusion(bf16[128,4096]{0,1:T(8,128)(2,1)S(1)} %bitcast.107, bf16[4096,1024]{1,0:T(8,128)(2,1)} %param.19), kind=kOutput, calls=%fused_computation.59 | convolution fusion | flops 1074003840 | bytes 9961984 | tf_op jit(solution)/shard_map/dot_general | solution.py:109
  81.7 3.0 %convolution_convert_fusion.1 = bf16[128,1024]{1,0:T(8,128)(2,1)} fusion(bf16[1024,1024]{1,0:T(8,128)(2,1)} %param.23, f32[128,1024]{1,0:T(8,128)} %copy-done.7, f32[1024]{0:T(1024)S(1)} %convert_element_type.60, f32[128]{0:T(128)S(1)} %add_rsqrt_fusion.1), kind=kOutput, calls=%fused_computation.52 | convolution fusion | flops 268959744 | bytes 2888192 | tf_op jit(solution)/shard_map/dot_general | solution.py:127
  85.1 3.2 %convolution_convert_fusion = bf16[512,1024]{1,0:T(8,128)(2,1)S(1)} fusion(bf16[1024,1024]{1,0:T(8,128)(2,1)} %param.21, bf16[1,512,1024]{2,1,0:T(8,128)(2,1)} %param.16), kind=kOutput, calls=%fused_computation.51 | convolution fusion | flops 1074266112 | bytes 4194304 | tf_op jit(solution)/shard_map/dot_general | solution.py:119
  88.3 2.4 reshape.137
  90.6 3.6 %copy.43 = bf16[2,256,16,64]{1,3,2,0:T(8,128)(2,1)} copy(bf16[2,256,16,64]{3,2,1,0:T(8,128)(2,1)} %reshape.137) | data formatting | bytes 2097152 | tf_op jit(solution)/shard_map/while | solution.py:74
  94.4 36.8 %all-gather.3.cloned.1.call-done = bf16[1024,1024]{1,0:T(8,128)(2,1)} async-done(((bf16[128,1024]{1,0:T(8,128)(2,1)}), bf16[1024,1024]{1,0:T(8,128)(2,1)}) %all-gather.3.cloned.1.call-update) | async-done | bytes 2097168 | tf_op jit(solution)/shard_map/all_gather | solution.py:134
  131.2 49.8 %all-gather.5.cloned.1.call-done = bf16[1024,1024]{1,0:T(8,128)(2,1)} async-done(((bf16[128,1024]{1,0:T(8,128)(2,1)}), bf16[1024,1024]{1,0:T(8,128)(2,1)}) %all-gather.5.cloned.1.call-update) | async-done | bytes 2097168 | tf_op jit(solution)/shard_map/all_gather | solution.py:135
  181.0 1.6 broadcast_in_dim.57
  182.5 87.3 %while.17 = (s32[]{:T(128)}, f32[2,16,256]{2,1,0:T(8,128)S(1)}, f32[2,16,256]{2,1,0:T(8,128)S(1)}, f32[2,16,256,64]{2,3,1,0:T(8,128)}, s32[1024]{0:T(1024)S(1)},...) while((s32[]{:T(128)}, f32[2,16,256]{2,1,0:T(8,128)S(1)}, ...), condition=%wide.region_12.13_spmd, body=%wide.region_3.12_spmd.sunk | while | flops 1130135552 | bytes 103557752 | solution.py:74
  185.6 3.1 %slice_bitcast_fusion.13 = (f32[16,256,64]{1,2,0:T(8,128)}, f32[16,256,64]{1,2,0:T(8,128)}) fusion(f32[2,16,256,64]{2,3,1,0:T(8,128)} %get-tuple-element.517), kind=kLoop, calls=%fused_computation.38.clone.1 | loop fusion | bytes 4194304 | tf_op jit(solution)/shard_map/while/body/eval_jaxpr/squeeze | solution.py:55
  188.7 3.0 %constant_dynamic-slice_fusion.3 = (bf16[512,1024]{1,0:T(8,128)(2,1)}, bf16[512,1024]{1,0:T(8,128)(2,1)}) fusion(bf16[1024,1024]{1,0:T(8,128)(2,1)} %get-tuple-element.535, s32[]{:T(128)S(6)} %select_n.71, bf16[1024,1024]{1,0:T(8,128)(2,1)} %get-tuple-element.534), kind=kLoop, calls=%fused_computation.45.clone.1 | loop fusion | bytes 4194308 | tf_op jit(solution)/shard_map/while/body/eval_jaxpr/dynamic_slice | solution.py:49
  191.7 1.5 copy.55
  193.9 2.3 copy.56
  196.2 11.9 %conditional.4 = (f32[1,16,256]{2,1,0:T(8,128)}, f32[1,16,256]{2,1,0:T(8,128)S(1)}, f32[1,16,256,64]{2,3,1,0:T(8,128)}) conditional(s32[]{:T(128)} %bitcast.95, (f32[16,256]{1,0:T(8,128)}, f32[16,256]{1,0:T(8,128)S(1)}, f32[16,256,64]{1,2,0:T(8,128)}) %tuple.133, (s32[512]{0:T(512)S(1)}, s32[256]{0:T(256)S(1)}, bf16[2,256,16,64]{1,3,2,0:T(8,128)(2,1)}, ...), branch_computations={%region_8.8_spmd, %region_9.0_spmd} | conditional | flops 564797440 | bytes 43224172 | solution.py:71
  196.4 2.9 %fusion.18 = (f32[16,256]{1,0:T(8,128)S(1)}, f32[16,256,512]{2,1,0:T(8,128)S(1)}) fusion(pred[256,512]{1,0:T(8,128)(4,1)S(1)} %broadcast_compare_fusion.1, bf16[512,16,64]{0,2,1:T(8,128)(2,1)S(1)} %get-tuple-element.254, bf16[2,256,16,64]{1,3,2,0:T(8,128)(2,1)} %get-tuple-element.253), kind=kOutput, calls=%fused_computation.20 | convolution fusion | flops 274722816 | bytes 10108928 | tf_op jit(solution)/shard_map/while/body/eval_jaxpr/cond/branch_1_fun/rhd,khd->hrk/dot_general | solution.py:22
  199.9 3.2 %fusion.20 = f32[16,256]{1,0:T(8,128)S(1)} fusion(f32[16,256,512]{2,1,0:T(8,128)S(1)} %get-tuple-element.378, f32[16,256]{1,0:T(8,128)} %max.5, pred[256,512]{1,0:T(8,128)(4,1)S(1)} %broadcast_compare_fusion.1), kind=kLoop, calls=%fused_computation.22 | loop fusion | flops 10481664 | bytes 8552448 | tf_op jit(solution)/shard_map/while/body/eval_jaxpr/cond/branch_1_fun/reduce_sum | solution.py:30
  203.9 3.2 %fusion.27 = f32[1,16,256,64]{2,3,1,0:T(8,128)S(1)} fusion(bf16[512,16,64]{0,2,1:T(8,128)(2,1)S(1)} %copy-done.5, f32[16,256,512]{2,1,0:T(8,128)S(1)} %get-tuple-element.378, f32[16,256]{1,0:T(8,128)} %max.5, pred[256,512]{1,0:T(8,128)(4,1)S(1)} %broadcast_compare_fusion.1, f32[16,256,64]{1,2,0:T(8,128)S(1)} %copy-done.3, f32[16,256]{1,0:T(8,128)S(1)} %get-tuple-element.374), kind=kOutput, calls=%fused_computation.26 | convolution fusion | flops 279445504 | bytes 11698176 | tf_op jit(solution)/shard_map/while/body/eval_jaxpr/cond/branch_1_fun/hrk,khd->hrd/dot_general | solution.py:31
  210.5 11.8 %conditional.5 = (f32[1,16,256]{2,1,0:T(8,128)}, f32[1,16,256]{2,1,0:T(8,128)S(1)}, f32[1,16,256,64]{2,3,1,0:T(8,128)}) conditional(s32[]{:T(128)} %bitcast.98, (f32[16,256]{1,0:T(8,128)}, f32[16,256]{1,0:T(8,128)S(1)}, f32[16,256,64]{1,2,0:T(8,128)}) %tuple.135, (s32[512]{0:T(512)S(1)}, s32[256]{0:T(256)S(1)}, bf16[2,256,16,64]{1,3,2,0:T(8,128)(2,1)}, ...), branch_computations={%region_4.4_spmd, %region_5.0_spmd} | conditional | flops 564797440 | bytes 43224172 | solution.py:71
  210.7 2.9 %fusion = (f32[16,256]{1,0:T(8,128)S(1)}, f32[16,256,512]{2,1,0:T(8,128)S(1)}) fusion(pred[256,512]{1,0:T(8,128)(4,1)S(1)} %broadcast_compare_fusion, bf16[512,16,64]{0,2,1:T(8,128)(2,1)S(1)} %get-tuple-element.246, bf16[2,256,16,64]{1,3,2,0:T(8,128)(2,1)} %get-tuple-element.245), kind=kOutput, calls=%fused_computation.2 | convolution fusion | flops 274722816 | bytes 10108928 | tf_op jit(solution)/shard_map/while/body/eval_jaxpr/cond/branch_1_fun/rhd,khd->hrk/dot_general | solution.py:22
  214.2 3.2 %fusion.2 = f32[16,256]{1,0:T(8,128)S(1)} fusion(f32[16,256,512]{2,1,0:T(8,128)S(1)} %get-tuple-element.376, f32[16,256]{1,0:T(8,128)} %max.4, pred[256,512]{1,0:T(8,128)(4,1)S(1)} %broadcast_compare_fusion), kind=kLoop, calls=%fused_computation.4 | loop fusion | flops 10481664 | bytes 8552448 | tf_op jit(solution)/shard_map/while/body/eval_jaxpr/cond/branch_1_fun/reduce_sum | solution.py:30
  218.2 3.2 %fusion.9 = f32[1,16,256,64]{2,3,1,0:T(8,128)S(1)} fusion(bf16[512,16,64]{0,2,1:T(8,128)(2,1)S(1)} %copy-done.6, f32[16,256,512]{2,1,0:T(8,128)S(1)} %get-tuple-element.376, f32[16,256]{1,0:T(8,128)} %max.4, pred[256,512]{1,0:T(8,128)(4,1)S(1)} %broadcast_compare_fusion, f32[16,256,64]{1,2,0:T(8,128)S(1)} %copy-done.1, f32[16,256]{1,0:T(8,128)S(1)} %get-tuple-element.372), kind=kOutput, calls=%fused_computation.8 | convolution fusion | flops 279445504 | bytes 11698176 | tf_op jit(solution)/shard_map/while/body/eval_jaxpr/cond/branch_1_fun/hrk,khd->hrd/dot_general | solution.py:31
  223.1 3.1 %pad_maximum_fusion.9 = f32[2,16,256,64]{2,3,1,0:T(8,128)} fusion(f32[1,16,256,64]{2,3,1,0:T(8,128)} %get-tuple-element.486, f32[1,16,256,64]{2,3,1,0:T(8,128)} %get-tuple-element.487), kind=kLoop, calls=%fused_computation.36.clone.1 | loop fusion | flops 524288 | bytes 4194304 | tf_op jit(solution)/shard_map/while/body/eval_jaxpr/stack | solution.py:72
  229.2 3.1 %slice_bitcast_fusion.13 = (f32[16,256,64]{1,2,0:T(8,128)}, f32[16,256,64]{1,2,0:T(8,128)}) fusion(f32[2,16,256,64]{2,3,1,0:T(8,128)} %get-tuple-element.517), kind=kLoop, calls=%fused_computation.38.clone.1 | loop fusion | bytes 4194304 | tf_op jit(solution)/shard_map/while/body/eval_jaxpr/squeeze | solution.py:55
  232.4 3.0 %constant_dynamic-slice_fusion.3 = (bf16[512,1024]{1,0:T(8,128)(2,1)}, bf16[512,1024]{1,0:T(8,128)(2,1)}) fusion(bf16[1024,1024]{1,0:T(8,128)(2,1)} %get-tuple-element.535, s32[]{:T(128)S(6)} %select_n.71, bf16[1024,1024]{1,0:T(8,128)(2,1)} %get-tuple-element.534), kind=kLoop, calls=%fused_computation.45.clone.1 | loop fusion | bytes 4194308 | tf_op jit(solution)/shard_map/while/body/eval_jaxpr/dynamic_slice | solution.py:49
  235.4 1.5 copy.55
  237.6 2.3 copy.56
  239.9 11.9 %conditional.4 = (f32[1,16,256]{2,1,0:T(8,128)}, f32[1,16,256]{2,1,0:T(8,128)S(1)}, f32[1,16,256,64]{2,3,1,0:T(8,128)}) conditional(s32[]{:T(128)} %bitcast.95, (f32[16,256]{1,0:T(8,128)}, f32[16,256]{1,0:T(8,128)S(1)}, f32[16,256,64]{1,2,0:T(8,128)}) %tuple.133, (s32[512]{0:T(512)S(1)}, s32[256]{0:T(256)S(1)}, bf16[2,256,16,64]{1,3,2,0:T(8,128)(2,1)}, ...), branch_computations={%region_8.8_spmd, %region_9.0_spmd} | conditional | flops 564797440 | bytes 43224172 | solution.py:71
  240.0 2.9 %fusion.18 = (f32[16,256]{1,0:T(8,128)S(1)}, f32[16,256,512]{2,1,0:T(8,128)S(1)}) fusion(pred[256,512]{1,0:T(8,128)(4,1)S(1)} %broadcast_compare_fusion.1, bf16[512,16,64]{0,2,1:T(8,128)(2,1)S(1)} %get-tuple-element.254, bf16[2,256,16,64]{1,3,2,0:T(8,128)(2,1)} %get-tuple-element.253), kind=kOutput, calls=%fused_computation.20 | convolution fusion | flops 274722816 | bytes 10108928 | tf_op jit(solution)/shard_map/while/body/eval_jaxpr/cond/branch_1_fun/rhd,khd->hrk/dot_general | solution.py:22
  243.6 3.2 %fusion.20 = f32[16,256]{1,0:T(8,128)S(1)} fusion(f32[16,256,512]{2,1,0:T(8,128)S(1)} %get-tuple-element.378, f32[16,256]{1,0:T(8,128)} %max.5, pred[256,512]{1,0:T(8,128)(4,1)S(1)} %broadcast_compare_fusion.1), kind=kLoop, calls=%fused_computation.22 | loop fusion | flops 10481664 | bytes 8552448 | tf_op jit(solution)/shard_map/while/body/eval_jaxpr/cond/branch_1_fun/reduce_sum | solution.py:30
  247.5 3.1 %fusion.27 = f32[1,16,256,64]{2,3,1,0:T(8,128)S(1)} fusion(bf16[512,16,64]{0,2,1:T(8,128)(2,1)S(1)} %copy-done.5, f32[16,256,512]{2,1,0:T(8,128)S(1)} %get-tuple-element.378, f32[16,256]{1,0:T(8,128)} %max.5, pred[256,512]{1,0:T(8,128)(4,1)S(1)} %broadcast_compare_fusion.1, f32[16,256,64]{1,2,0:T(8,128)S(1)} %copy-done.3, f32[16,256]{1,0:T(8,128)S(1)} %get-tuple-element.374), kind=kOutput, calls=%fused_computation.26 | convolution fusion | flops 279445504 | bytes 11698176 | tf_op jit(solution)/shard_map/while/body/eval_jaxpr/cond/branch_1_fun/hrk,khd->hrd/dot_general | solution.py:31
  254.2 11.8 %conditional.5 = (f32[1,16,256]{2,1,0:T(8,128)}, f32[1,16,256]{2,1,0:T(8,128)S(1)}, f32[1,16,256,64]{2,3,1,0:T(8,128)}) conditional(s32[]{:T(128)} %bitcast.98, (f32[16,256]{1,0:T(8,128)}, f32[16,256]{1,0:T(8,128)S(1)}, f32[16,256,64]{1,2,0:T(8,128)}) %tuple.135, (s32[512]{0:T(512)S(1)}, s32[256]{0:T(256)S(1)}, bf16[2,256,16,64]{1,3,2,0:T(8,128)(2,1)}, ...), branch_computations={%region_4.4_spmd, %region_5.0_spmd} | conditional | flops 564797440 | bytes 43224172 | solution.py:71
  254.4 2.9 %fusion = (f32[16,256]{1,0:T(8,128)S(1)}, f32[16,256,512]{2,1,0:T(8,128)S(1)}) fusion(pred[256,512]{1,0:T(8,128)(4,1)S(1)} %broadcast_compare_fusion, bf16[512,16,64]{0,2,1:T(8,128)(2,1)S(1)} %get-tuple-element.246, bf16[2,256,16,64]{1,3,2,0:T(8,128)(2,1)} %get-tuple-element.245), kind=kOutput, calls=%fused_computation.2 | convolution fusion | flops 274722816 | bytes 10108928 | tf_op jit(solution)/shard_map/while/body/eval_jaxpr/cond/branch_1_fun/rhd,khd->hrk/dot_general | solution.py:22
  257.9 3.2 %fusion.2 = f32[16,256]{1,0:T(8,128)S(1)} fusion(f32[16,256,512]{2,1,0:T(8,128)S(1)} %get-tuple-element.376, f32[16,256]{1,0:T(8,128)} %max.4, pred[256,512]{1,0:T(8,128)(4,1)S(1)} %broadcast_compare_fusion), kind=kLoop, calls=%fused_computation.4 | loop fusion | flops 10481664 | bytes 8552448 | tf_op jit(solution)/shard_map/while/body/eval_jaxpr/cond/branch_1_fun/reduce_sum | solution.py:30
  261.9 3.2 %fusion.9 = f32[1,16,256,64]{2,3,1,0:T(8,128)S(1)} fusion(bf16[512,16,64]{0,2,1:T(8,128)(2,1)S(1)} %copy-done.6, f32[16,256,512]{2,1,0:T(8,128)S(1)} %get-tuple-element.376, f32[16,256]{1,0:T(8,128)} %max.4, pred[256,512]{1,0:T(8,128)(4,1)S(1)} %broadcast_compare_fusion, f32[16,256,64]{1,2,0:T(8,128)S(1)} %copy-done.1, f32[16,256]{1,0:T(8,128)S(1)} %get-tuple-element.372), kind=kOutput, calls=%fused_computation.8 | convolution fusion | flops 279445504 | bytes 11698176 | tf_op jit(solution)/shard_map/while/body/eval_jaxpr/cond/branch_1_fun/hrk,khd->hrd/dot_general | solution.py:31
  266.8 3.1 %pad_maximum_fusion.9 = f32[2,16,256,64]{2,3,1,0:T(8,128)} fusion(f32[1,16,256,64]{2,3,1,0:T(8,128)} %get-tuple-element.486, f32[1,16,256,64]{2,3,1,0:T(8,128)} %get-tuple-element.487), kind=kLoop, calls=%fused_computation.36.clone.1 | loop fusion | flops 524288 | bytes 4194304 | tf_op jit(solution)/shard_map/while/body/eval_jaxpr/stack | solution.py:72
  269.9 1.8 fusion.38
  273.1 2.6 multiply_reduce_fusion
  275.7 1.2 fusion.36
  (87 shorter events, 23.9 us)
Async XLA Ops:
  6.5 266.5 %copy-start = (bf16[1024,1024]{1,0:T(8,128)(2,1)S(1)}, bf16[1024,1024]{1,0:T(8,128)(2,1)}, u32[]{:S(2)}) copy-start(bf16[1024,1024]{1,0:T(8,128)(2,1)} %param.24) | copy-start | bytes 6291460
  6.5 37.8 %copy-start.10 = (bf16[1024]{0:T(1024)(128)(2,1)S(1)}, bf16[1024]{0:T(1024)(128)(2,1)}, u32[]{:S(2)}) copy-start(bf16[1024]{0:T(1024)(128)(2,1)} %param.20) | copy-start | bytes 6148
  38.2 28.5 %all-to-all-start.1 = ((bf16[8,2,32768]{2,1,0:T(2,128)(2,1)}), bf16[8,2,32768]{2,1,0:T(2,128)(2,1)S(1)}, u32[]{:S(2)}, u32[]{:S(2)}) async-start(bf16[8,2,32768]{2,1,0:T(2,128)(2,1)} %reshape.139), calls=%async_computation.1 | async-start | bytes 2097152 | tf_op jit(solution)/shard_map/all_to_all | solution.py:94
  44.4 86.8 %all-gather.3.cloned.1.call-start = ((), (), s32[]{:S(2)}) async-start(), calls=%async_computation.2 | async-start | bytes 2359296 | tf_op jit(solution)/shard_map/all_gather | solution.py:134
  74.6 5.7 %copy-start.8 = (bf16[1024,1024]{1,0:T(8,128)(2,1)S(1)}, bf16[1024,1024]{1,0:T(8,128)(2,1)}, u32[]{:S(2)}) copy-start(bf16[1024,1024]{1,0:T(8,128)(2,1)} %param.22) | copy-start | bytes 6291460
  74.6 10.1 %copy-start.9 = (s32[1,1024]{1,0:T(1,128)S(1)}, s32[1,1024]{1,0:T(1,128)}, u32[]{:S(2)}) copy-start(s32[1,1024]{1,0:T(1,128)} %param.18) | copy-start | bytes 12292
  79.5 0.8 copy-start.7
  81.5 12.7 %copy-start.11 = (bf16[1024]{0:T(1024)(128)(2,1)S(1)}, bf16[1024]{0:T(1024)(128)(2,1)}, u32[]{:S(2)}) copy-start(bf16[1024]{0:T(1024)(128)(2,1)} %param.25) | copy-start | bytes 6148
  81.5 99.5 %all-gather.5.cloned.1.call-start = ((), (), s32[]{:S(2)}) async-start(), calls=%async_computation.3 | async-start | bytes 2359296 | tf_op jit(solution)/shard_map/all_gather | solution.py:135
  196.3 7.5 %copy-start.3 = (f32[16,256,64]{1,2,0:T(8,128)S(1)}, f32[16,256,64]{1,2,0:T(8,128)}, u32[]{:S(2)}) copy-start(f32[16,256,64]{1,2,0:T(8,128)} %get-tuple-element.256) | copy-start | bytes 3145732 | tf_op jit(solution)/shard_map/while/body/eval_jaxpr/cond
  196.3 7.5 %copy-start.5 = (bf16[512,16,64]{0,2,1:T(8,128)(2,1)S(1)}, bf16[512,16,64]{0,2,1:T(8,128)(2,1)}, u32[]{:S(2)}) copy-start(bf16[512,16,64]{0,2,1:T(8,128)(2,1)} %get-tuple-element.257) | copy-start | bytes 3145732 | tf_op jit(solution)/shard_map/while/body/eval_jaxpr/cond
  207.0 1.0 copy-start.4
  210.7 7.5 %copy-start.1 = (f32[16,256,64]{1,2,0:T(8,128)S(1)}, f32[16,256,64]{1,2,0:T(8,128)}, u32[]{:S(2)}) copy-start(f32[16,256,64]{1,2,0:T(8,128)} %get-tuple-element.248) | copy-start | bytes 3145732 | tf_op jit(solution)/shard_map/while/body/eval_jaxpr/cond
  210.7 7.5 %copy-start.6 = (bf16[512,16,64]{0,2,1:T(8,128)(2,1)S(1)}, bf16[512,16,64]{0,2,1:T(8,128)(2,1)}, u32[]{:S(2)}) copy-start(bf16[512,16,64]{0,2,1:T(8,128)(2,1)} %get-tuple-element.249) | copy-start | bytes 3145732 | tf_op jit(solution)/shard_map/while/body/eval_jaxpr/cond
  221.4 1.0 copy-start.2
  240.0 7.5 %copy-start.3 = (f32[16,256,64]{1,2,0:T(8,128)S(1)}, f32[16,256,64]{1,2,0:T(8,128)}, u32[]{:S(2)}) copy-start(f32[16,256,64]{1,2,0:T(8,128)} %get-tuple-element.256) | copy-start | bytes 3145732 | tf_op jit(solution)/shard_map/while/body/eval_jaxpr/cond
  240.0 7.5 %copy-start.5 = (bf16[512,16,64]{0,2,1:T(8,128)(2,1)S(1)}, bf16[512,16,64]{0,2,1:T(8,128)(2,1)}, u32[]{:S(2)}) copy-start(bf16[512,16,64]{0,2,1:T(8,128)(2,1)} %get-tuple-element.257) | copy-start | bytes 3145732 | tf_op jit(solution)/shard_map/while/body/eval_jaxpr/cond
  250.7 1.0 copy-start.4
  254.4 7.5 %copy-start.1 = (f32[16,256,64]{1,2,0:T(8,128)S(1)}, f32[16,256,64]{1,2,0:T(8,128)}, u32[]{:S(2)}) copy-start(f32[16,256,64]{1,2,0:T(8,128)} %get-tuple-element.248) | copy-start | bytes 3145732 | tf_op jit(solution)/shard_map/while/body/eval_jaxpr/cond
  254.4 7.5 %copy-start.6 = (bf16[512,16,64]{0,2,1:T(8,128)(2,1)S(1)}, bf16[512,16,64]{0,2,1:T(8,128)(2,1)}, u32[]{:S(2)}) copy-start(bf16[512,16,64]{0,2,1:T(8,128)(2,1)} %get-tuple-element.249) | copy-start | bytes 3145732 | tf_op jit(solution)/shard_map/while/body/eval_jaxpr/cond
  265.1 1.0 copy-start.2
Sparse Core Ops, SparseCore 0:
  81.6 49.5 all-gather.2
  133.3 47.6 all-gather.4
